TPU v7x, 512 devices: a whole 4x8x8 slice. The times are simulated.
512 devices in a mesh: section: 4 (over z_hi), row: 4 (over z_lo, core), col: 32 (over y, x).
Axes of the slice: x: 4, y: 8, z: 8 (z_hi: 4, z_lo: 2; z = z_hi * 2 + z_lo), core: 2. Of those that a mesh axis runs over, the one named last changes fastest.
Arguments:
- state: bfloat16 [4, 128, 1024, 256], P('section', 'row', 'col'), may hold values from -6 to 6
- fresh: bfloat16 [128, 1024, 256], P('row', 'col'), may hold values from -6 to 6
- conv_first: bfloat16 [4, 3, 3, 256, 256], P('section'), may hold values from -0.125 to 0.125
- conv_second: bfloat16 [4, 3, 3, 256, 256], P('section'), may hold values from -0.125 to 0.125
- gains: float32 [4, 2, 256], P('section'), may hold values from 0.1 to 1.9
- shifts: float32 [4, 2, 256], P('section'), may hold values from -2.4 to 2.4
Outputs:
- blocks: bfloat16 [2, 4, 128, 1024, 256], P(None, 'section', 'row', 'col')
All inputs are finite; a program needn't handle non-finite values.
Results may differ from a plain program's by a relative error of at most 0.005.
Values may be sent and summed in bfloat16 or wider, within the bound.
No kernel may reach another device: no remote copies, remote signals or barrier semaphores. Data moves between devices by JAX's collectives and lax.ppermute only.
A program may use at most 64 MiB of HBM per device.

v0:
```python
import jax
import jax.numpy as jnp
from jax import lax
from jax.sharding import PartitionSpec as P

TICKS = 2


def extended(block, sides, width):
    for axis, dim in sides:
        count = lax.axis_size(axis)
        forward = [(i, i + 1) for i in range(count - 1)]
        backward = [(target, source) for source, target in forward]
        low = lax.ppermute(
            lax.slice_in_dim(block, block.shape[dim] - width, None, axis=dim), axis, forward
        )
        high = lax.ppermute(lax.slice_in_dim(block, 0, width, axis=dim), axis, backward)
        block = jnp.concatenate([low, block, high], axis=dim)
    return block


def shifted(x, axis, by):
    devices = lax.axis_size(axis)
    pairs = [(i, i + by) for i in range(devices) if 0 <= i + by < devices]
    return lax.ppermute(x, axis, pairs)


def convolve(padded, kernel):
    out_rows = padded.shape[0] - 2
    out_cols = padded.shape[1] - 2
    channels = padded.shape[2]
    stacked = jnp.concatenate(
        [padded[:, col_tap : col_tap + out_cols] for col_tap in range(3)], axis=2
    )
    summed = jnp.zeros((out_rows * out_cols, kernel.shape[3]), jnp.float32)
    for row_tap in range(3):
        summed = summed + jnp.dot(
            stacked[row_tap : row_tap + out_rows].reshape(out_rows * out_cols, 3 * channels),
            kernel[row_tap].reshape(3 * channels, kernel.shape[3]),
            preferred_element_type=jnp.float32,
        )
    return summed.reshape(out_rows, out_cols, kernel.shape[3])


def section_block(features, first_kernel, second_kernel, gain_pair, shift_pair):
    tile_rows = features.shape[0]
    tile_cols = features.shape[1]
    widened = extended(features, (("row", 0), ("col", 1)), 2)
    first_out = convolve(widened, first_kernel)
    row_ids = lax.axis_index("row") * tile_rows - 1 + lax.iota(jnp.int32, tile_rows + 2)
    col_ids = lax.axis_index("col") * tile_cols - 1 + lax.iota(jnp.int32, tile_cols + 2)
    row_inside = (row_ids >= 0) & (row_ids < tile_rows * lax.axis_size("row"))
    col_inside = (col_ids >= 0) & (col_ids < tile_cols * lax.axis_size("col"))
    inside = row_inside[:, None, None] & col_inside[None, :, None]
    hidden = jnp.where(inside, jax.nn.relu(gain_pair[0] * first_out + shift_pair[0]), 0.0).astype(
        jnp.bfloat16
    )
    second_out = convolve(hidden, second_kernel)
    summed = features.astype(jnp.float32) + gain_pair[1] * second_out + shift_pair[1]
    return jax.nn.relu(summed).astype(jnp.bfloat16)


def per_device(state, fresh, conv_first, conv_second, gains, shifts):
    features = state[0]
    results = []
    for tick_index in range(TICKS):
        output = section_block(features, conv_first[0], conv_second[0], gains[0], shifts[0])
        results.append(output)
        if tick_index + 1 < TICKS:
            arrived = shifted(output, "section", 1)
            features = jnp.where(lax.axis_index("section") == 0, fresh, arrived)
    return jnp.stack(results)[:, None]


def solution(mesh):
    in_specs = (
        P("section", "row", "col", None),
        P("row", "col", None),
        P("section", None, None, None, None),
        P("section", None, None, None, None),
        P("section", None, None),
        P("section", None, None),
    )
    out_specs = P(None, "section", "row", "col", None)
    return jax.shard_map(
        per_device, mesh=mesh, in_specs=in_specs, out_specs=out_specs, check_vma=False
    )
```

profile of v0, /device:TPU:159, one launch (start us, length us, event | category | flops | bytes accessed | tf_op | source)
XLA Modules:
  0.0 118.4 jit_solution(10476405314100446345)
XLA Ops:
  0.0 0.9 slice_bitcast_fusion.1
  0.9 4.5 %collective-permute-start = (bf16[2,32,256]{2,1,0:T(8,128)(2,1)S(1)}, bf16[2,32,256]{2,1,0:T(8,128)(2,1)S(1)}, u32[]{:S(2)}, u32[]{:S(2)}) collective-permute-start(bf16[2,32,256]{2,1,0:T(8,128)(2,1)S(1)} %get-tuple-element.35), channel_id=1, source_target_pairs={{0,32},{32,64},{64,96},{1,33},{33,65},{65,97},{2,34},{34,66},{66,9... | collective-permute-start | bytes 98312 | tf_op jit(solution)/shard_map/ppermute | solution.py:14
  5.4 1.9 %collective-permute-start.1 = (bf16[2,32,256]{2,1,0:T(8,128)(2,1)S(1)}, bf16[2,32,256]{2,1,0:T(8,128)(2,1)S(1)}, u32[]{:S(2)}, u32[]{:S(2)}) collective-permute-start(bf16[2,32,256]{2,1,0:T(8,128)(2,1)S(1)} %get-tuple-element.36), channel_id=1, source_target_pairs={{32,0},{64,32},{96,64},{33,1},{65,33},{97,65},{34,2},{66,34},{98,6... | collective-permute-start | bytes 98312 | tf_op jit(solution)/shard_map/ppermute | solution.py:17
  7.4 2.1 %fusion.10 = (bf16[1,1,3,256,256]{4,3,2,1,0:T(8,128)(2,1)}, bf16[1,1,3,256,256]{4,3,2,1,0:T(8,128)(2,1)S(1)}, bf16[1,1,3,256,256]{4,3,2,1,0:T(8,128)(2,1)S(1)}) fusion(bf16[1,3,3,256,256]{4,3,2,1,0:T(8,128)(2,1)} %param.8), kind=kLoop, calls=%fused_computation.46 | loop fusion | bytes 2359296 | tf_op jit(solution)/shard_map/slice | solution.py:39
  9.5 1.1 fusion.9
  10.7 0.1 broadcast_and_fusion
  10.8 0.1 pad_maximum_fusion.15
  10.9 4.3 %collective-permute-start.2 = (bf16[36,2,256]{2,1,0:T(2,128)(2,1)S(1)}, bf16[36,2,256]{2,1,0:T(2,128)(2,1)S(1)}, u32[]{:S(2)}, u32[]{:S(2)}) collective-permute-start(bf16[36,2,256]{2,1,0:T(2,128)(2,1)S(1)} %get-tuple-element.31), channel_id=1, source_target_pairs={{0,1},{1,2},{2,3},{3,4},{4,5},{5,6},{6,7},{7,8},{8,9},{9,10},{10,1... | collective-permute-start | bytes 110600 | tf_op jit(solution)/shard_map/ppermute | solution.py:14
  15.2 1.9 %collective-permute-start.3 = (bf16[36,2,256]{2,1,0:T(2,128)(2,1)S(1)}, bf16[36,2,256]{2,1,0:T(2,128)(2,1)S(1)}, u32[]{:S(2)}, u32[]{:S(2)}) collective-permute-start(bf16[36,2,256]{2,1,0:T(2,128)(2,1)S(1)} %get-tuple-element.32), channel_id=1, source_target_pairs={{1,0},{2,1},{3,2},{4,3},{5,4},{6,5},{7,6},{8,7},{9,8},{10,9},{11,1... | collective-permute-start | bytes 110600 | tf_op jit(solution)/shard_map/ppermute | solution.py:17
  17.2 6.1 %collective-permute-done.3 = bf16[36,2,256]{2,1,0:T(2,128)(2,1)S(1)} collective-permute-done((bf16[36,2,256]{2,1,0:T(2,128)(2,1)S(1)}, bf16[36,2,256]{2,1,0:T(2,128)(2,1)S(1)}, u32[]{:S(2)}, u32[]{:S(2)}) %collective-permute-start.3) | collective-permute-done | bytes 36896 | tf_op jit(solution)/shard_map/ppermute | solution.py:17
  23.2 3.4 %fusion.3 = bf16[36,34,768]{2,1,0:T(8,128)(2,1)S(1)} fusion(bf16[36,2,256]{2,1,0:T(2,128)(2,1)S(1)} %collective-permute-done.3, bf16[36,2,256]{2,1,0:T(2,128)(2,1)S(1)} %collective-permute-done.2, bf16[2,32,256]{2,1,0:T(8,128)(2,1)S(1)} %collective-permute-done.1, bf16[32,32,256]{2,1,0:T(8,128)(2,1)S(1)} %bitcast.56, ...), kind=kLoop, calls=%fused_computation.12 | loop fusion | flops 24440832 | bytes 2543616 | tf_op jit(solution)/shard_map/concatenate | solution.py:32
  26.6 2.4 %fusion.6 = (bf16[34,34,768]{2,1,0:T(8,128)(2,1)}, bf16[34,34,768]{2,1,0:T(8,128)(2,1)S(1)}, bf16[34,34,768]{2,1,0:T(8,128)(2,1)}) fusion(bf16[36,34,768]{2,1,0:T(8,128)(2,1)S(1)} %fusion.3), kind=kLoop, calls=%fused_computation.42 | loop fusion | bytes 10653696 | tf_op jit(solution)/shard_map/slice | solution.py:38
  29.0 3.8 %reshape.130 = bf16[1156,768]{1,0:T(8,128)(2,1)} reshape(bf16[34,34,768]{2,1,0:T(8,128)(2,1)} %get-tuple-element.8) | data formatting | bytes 3551232 | tf_op jit(solution)/shard_map/reshape | solution.py:38
  32.8 1.7 %reshape.129 = bf16[1156,768]{1,0:T(8,128)(2,1)} reshape(bf16[34,34,768]{2,1,0:T(8,128)(2,1)S(1)} %get-tuple-element.9) | data formatting | bytes 3551232 | tf_op jit(solution)/shard_map/reshape | solution.py:38
  34.5 2.5 %reshape.128 = bf16[1156,768]{1,0:T(8,128)(2,1)S(1)} reshape(bf16[34,34,768]{2,1,0:T(8,128)(2,1)} %get-tuple-element.10) | data formatting | bytes 3551232 | tf_op jit(solution)/shard_map/reshape | solution.py:38
  37.1 0.6 fusion.16
  37.7 0.8 copy-done.4
  38.6 0.7 convolution_add_fusion.3
  39.2 0.8 copy-done.2
  40.1 0.7 convolution_add_fusion.2
  40.8 0.1 reshape.131
  40.9 0.4 select_convert_fusion.1
  41.3 0.4 fusion.12
  41.7 0.1 pad_maximum_fusion.8
  41.8 0.6 fusion.8
  42.4 0.4 copy-done.5
  42.8 0.6 fusion.17
  43.5 0.6 convolution_add_fusion.7
  44.1 0.4 copy-done.7
  44.5 0.6 convolution_add_fusion.6
  45.1 0.2 maximum_convert_fusion.1
  45.3 6.1 %collective-permute-start.4 = (bf16[32,32,256]{2,1,0:T(8,128)(2,1)S(1)}, bf16[32,32,256]{2,1,0:T(8,128)(2,1)}, u32[]{:S(2)}, u32[]{:S(2)}) collective-permute-start(bf16[32,32,256]{2,1,0:T(8,128)(2,1)S(1)} %maximum_convert_fusion.1), channel_id=1, source_target_pairs={{0,128},{128,256},{256,384},{1,129},{129,257},{257,385},{2,130},{1... | collective-permute-start | bytes 1572872 | tf_op jit(solution)/shard_map/ppermute | solution.py:25
  51.4 22.2 %collective-permute-done.4 = bf16[32,32,256]{2,1,0:T(8,128)(2,1)} collective-permute-done((bf16[32,32,256]{2,1,0:T(8,128)(2,1)S(1)}, bf16[32,32,256]{2,1,0:T(8,128)(2,1)}, u32[]{:S(2)}, u32[]{:S(2)}) %collective-permute-start.4) | collective-permute-done | bytes 524320 | tf_op jit(solution)/shard_map/ppermute | solution.py:25
  73.6 1.1 broadcast_select_fusion
  74.7 2.2 %collective-permute-start.5 = (bf16[2,32,256]{2,1,0:T(8,128)(2,1)S(1)}, bf16[2,32,256]{2,1,0:T(8,128)(2,1)S(1)}, u32[]{:S(2)}, u32[]{:S(2)}) collective-permute-start(bf16[2,32,256]{2,1,0:T(8,128)(2,1)S(1)} %get-tuple-element.33), channel_id=1, source_target_pairs={{0,32},{32,64},{64,96},{1,33},{33,65},{65,97},{2,34},{34,66},{66,9... | collective-permute-start | bytes 98312 | tf_op jit(solution)/shard_map/ppermute | solution.py:14
  76.9 2.1 %collective-permute-start.6 = (bf16[2,32,256]{2,1,0:T(8,128)(2,1)S(1)}, bf16[2,32,256]{2,1,0:T(8,128)(2,1)S(1)}, u32[]{:S(2)}, u32[]{:S(2)}) collective-permute-start(bf16[2,32,256]{2,1,0:T(8,128)(2,1)S(1)} %get-tuple-element.34), channel_id=1, source_target_pairs={{32,0},{64,32},{96,64},{33,1},{65,33},{97,65},{34,2},{66,34},{98,6... | collective-permute-start | bytes 98312 | tf_op jit(solution)/shard_map/ppermute | solution.py:17
  79.0 3.1 %collective-permute-done.6 = bf16[2,32,256]{2,1,0:T(8,128)(2,1)S(1)} collective-permute-done((bf16[2,32,256]{2,1,0:T(8,128)(2,1)S(1)}, bf16[2,32,256]{2,1,0:T(8,128)(2,1)S(1)}, u32[]{:S(2)}, u32[]{:S(2)}) %collective-permute-start.6) | collective-permute-done | bytes 32800 | tf_op jit(solution)/shard_map/ppermute | solution.py:17
  82.2 1.9 %collective-permute-start.7 = (bf16[36,2,256]{2,1,0:T(2,128)(2,1)S(1)}, bf16[36,2,256]{2,1,0:T(2,128)(2,1)S(1)}, u32[]{:S(2)}, u32[]{:S(2)}) collective-permute-start(bf16[36,2,256]{2,1,0:T(2,128)(2,1)S(1)} %get-tuple-element.29), channel_id=1, source_target_pairs={{0,1},{1,2},{2,3},{3,4},{4,5},{5,6},{6,7},{7,8},{8,9},{9,10},{10,1... | collective-permute-start | bytes 110600 | tf_op jit(solution)/shard_map/ppermute | solution.py:14
  84.1 3.5 %collective-permute-start.8 = (bf16[36,2,256]{2,1,0:T(2,128)(2,1)S(1)}, bf16[36,2,256]{2,1,0:T(2,128)(2,1)S(1)}, u32[]{:S(2)}, u32[]{:S(2)}) collective-permute-start(bf16[36,2,256]{2,1,0:T(2,128)(2,1)S(1)} %get-tuple-element.30), channel_id=1, source_target_pairs={{1,0},{2,1},{3,2},{4,3},{5,4},{6,5},{7,6},{8,7},{9,8},{10,9},{11,1... | collective-permute-start | bytes 110600 | tf_op jit(solution)/shard_map/ppermute | solution.py:17
  87.7 1.0 maximum_convert_fusion.2
  88.7 3.5 %collective-permute-done.8 = bf16[36,2,256]{2,1,0:T(2,128)(2,1)S(1)} collective-permute-done((bf16[36,2,256]{2,1,0:T(2,128)(2,1)S(1)}, bf16[36,2,256]{2,1,0:T(2,128)(2,1)S(1)}, u32[]{:S(2)}, u32[]{:S(2)}) %collective-permute-start.8) | collective-permute-done | bytes 36896 | tf_op jit(solution)/shard_map/ppermute | solution.py:17
  92.1 3.4 %fusion.1 = bf16[36,34,768]{2,1,0:T(8,128)(2,1)S(1)} fusion(bf16[36,2,256]{2,1,0:T(2,128)(2,1)S(1)} %collective-permute-done.8, bf16[36,2,256]{2,1,0:T(2,128)(2,1)S(1)} %collective-permute-done.7, bf16[2,32,256]{2,1,0:T(8,128)(2,1)S(1)} %collective-permute-done.6, bf16[32,32,256]{2,1,0:T(8,128)(2,1)S(1)} %broadcast_select_fusion, ...), kind=kLoop, calls=%fused_computation.6 | loop fusion | flops 24440832 | bytes 2543616 | tf_op jit(solution)/shard_map/concatenate | solution.py:32
  95.6 2.4 %fusion.5 = (bf16[34,34,768]{2,1,0:T(8,128)(2,1)}, bf16[34,34,768]{2,1,0:T(8,128)(2,1)S(1)}, bf16[34,34,768]{2,1,0:T(8,128)(2,1)}) fusion(bf16[36,34,768]{2,1,0:T(8,128)(2,1)S(1)} %fusion.1), kind=kLoop, calls=%fused_computation.41 | loop fusion | bytes 10653696 | tf_op jit(solution)/shard_map/slice | solution.py:38
  97.9 3.8 %reshape.139 = bf16[1156,768]{1,0:T(8,128)(2,1)} reshape(bf16[34,34,768]{2,1,0:T(8,128)(2,1)} %get-tuple-element.5) | data formatting | bytes 3551232 | tf_op jit(solution)/shard_map/reshape | solution.py:38
  101.7 1.7 %reshape.138 = bf16[1156,768]{1,0:T(8,128)(2,1)} reshape(bf16[34,34,768]{2,1,0:T(8,128)(2,1)S(1)} %get-tuple-element.6) | data formatting | bytes 3551232 | tf_op jit(solution)/shard_map/reshape | solution.py:38
  103.4 2.5 %reshape.137 = bf16[1156,768]{1,0:T(8,128)(2,1)S(1)} reshape(bf16[34,34,768]{2,1,0:T(8,128)(2,1)} %get-tuple-element.7) | data formatting | bytes 3551232 | tf_op jit(solution)/shard_map/reshape | solution.py:38
  106.0 0.6 fusion.18
  106.6 0.8 copy-done.3
  107.5 0.7 convolution_add_fusion.1
  108.2 0.8 copy-done.1
  109.1 1.7 %convolution_add_fusion = f32[1156,256]{1,0:T(8,128)} fusion(f32[1156,256]{1,0:T(8,128)S(1)} %convolution_add_fusion.1, bf16[1156,768]{1,0:T(8,128)(2,1)S(1)} %copy-done.1, bf16[768,256]{1,0:T(8,128)(2,1)S(1)} %bitcast.73), kind=kOutput, calls=%fused_computation | convolution fusion | flops 454853632 | bytes 4536320 | tf_op jit(solution)/shard_map/dot_general | solution.py:37
  110.8 1.4 %reshape.140 = f32[34,34,256]{2,1,0:T(8,128)S(1)} reshape(f32[1156,256]{1,0:T(8,128)} %convolution_add_fusion) | data formatting | bytes 2367488 | tf_op jit(solution)/shard_map/reshape | solution.py:42
  112.2 0.4 select_convert_fusion
  112.5 0.4 fusion.11
  112.9 0.1 pad_maximum_fusion.9
  113.1 0.6 fusion.7
  113.7 0.4 copy-done.6
  114.1 0.6 fusion.19
  114.7 0.6 convolution_add_fusion.5
  115.3 0.4 copy-done.8
  115.7 0.6 convolution_add_fusion.4
  116.3 0.2 fusion.4
  116.5 0.8 copy-done.15
  117.3 1.1 maximum_bitcast_fusion
  (41 shorter events, 0.4 us)
Async XLA Ops:
  0.0 9.5 %copy-start.16 = (bf16[1,3,3,256,256]{4,3,2,1,0:T(8,128)(2,1)S(1)}, bf16[1,3,3,256,256]{4,3,2,1,0:T(8,128)(2,1)}, u32[]{:S(2)}) copy-start(bf16[1,3,3,256,256]{4,3,2,1,0:T(8,128)(2,1)} %param.9) | copy-start | bytes 3538948
  0.9 9.9 %collective-permute-start = (bf16[2,32,256]{2,1,0:T(8,128)(2,1)S(1)}, bf16[2,32,256]{2,1,0:T(8,128)(2,1)S(1)}, u32[]{:S(2)}, u32[]{:S(2)}) collective-permute-start(bf16[2,32,256]{2,1,0:T(8,128)(2,1)S(1)} %get-tuple-element.35), channel_id=1, source_target_pairs={{0,32},{32,64},{64,96},{1,33},{33,65},{65,97},{2,34},{34,66},{66,9... | collective-permute-start | bytes 98312 | tf_op jit(solution)/shard_map/ppermute | solution.py:14
  5.4 5.3 %collective-permute-start.1 = (bf16[2,32,256]{2,1,0:T(8,128)(2,1)S(1)}, bf16[2,32,256]{2,1,0:T(8,128)(2,1)S(1)}, u32[]{:S(2)}, u32[]{:S(2)}) collective-permute-start(bf16[2,32,256]{2,1,0:T(8,128)(2,1)S(1)} %get-tuple-element.36), channel_id=1, source_target_pairs={{32,0},{64,32},{96,64},{33,1},{65,33},{97,65},{34,2},{66,34},{98,6... | collective-permute-start | bytes 98312 | tf_op jit(solution)/shard_map/ppermute | solution.py:17
  7.4 3.4 %copy-start.18 = (f32[1,2,256]{2,1,0:T(2,128)S(1)}, f32[1,2,256]{2,1,0:T(2,128)}, u32[]{:S(2)}) copy-start(f32[1,2,256]{2,1,0:T(2,128)} %param.10) | copy-start | bytes 6148
  7.4 3.4 %copy-start = (bf16[1,32,32,256]{3,2,1,0:T(8,128)(2,1)S(1)}, bf16[1,32,32,256]{3,2,1,0:T(8,128)(2,1)}, u32[]{:S(2)}) copy-start(bf16[1,32,32,256]{3,2,1,0:T(8,128)(2,1)} %param.6) | copy-start | bytes 1572868
  9.5 28.2 %copy-start.13 = (bf16[1,1,3,256,256]{4,3,2,1,0:T(8,128)(2,1)}, bf16[1,1,3,256,256]{4,3,2,1,0:T(8,128)(2,1)S(1)}, u32[]{:S(2)}) copy-start(bf16[1,1,3,256,256]{4,3,2,1,0:T(8,128)(2,1)S(1)} %get-tuple-element.22) | copy-start | bytes 1179652
  9.5 7.6 %copy-start.19 = (f32[1,2,256]{2,1,0:T(2,128)S(1)}, f32[1,2,256]{2,1,0:T(2,128)}, u32[]{:S(2)}) copy-start(f32[1,2,256]{2,1,0:T(2,128)} %param.11) | copy-start | bytes 6148
  10.9 6.3 %collective-permute-start.2 = (bf16[36,2,256]{2,1,0:T(2,128)(2,1)S(1)}, bf16[36,2,256]{2,1,0:T(2,128)(2,1)S(1)}, u32[]{:S(2)}, u32[]{:S(2)}) collective-permute-start(bf16[36,2,256]{2,1,0:T(2,128)(2,1)S(1)} %get-tuple-element.31), channel_id=1, source_target_pairs={{0,1},{1,2},{2,3},{3,4},{4,5},{5,6},{6,7},{7,8},{8,9},{9,10},{10,1... | collective-permute-start | bytes 110600 | tf_op jit(solution)/shard_map/ppermute | solution.py:14
  15.2 8.0 %collective-permute-start.3 = (bf16[36,2,256]{2,1,0:T(2,128)(2,1)S(1)}, bf16[36,2,256]{2,1,0:T(2,128)(2,1)S(1)}, u32[]{:S(2)}, u32[]{:S(2)}) collective-permute-start(bf16[36,2,256]{2,1,0:T(2,128)(2,1)S(1)} %get-tuple-element.32), channel_id=1, source_target_pairs={{1,0},{2,1},{3,2},{4,3},{5,4},{6,5},{7,6},{8,7},{9,8},{10,9},{11,1... | collective-permute-start | bytes 110600 | tf_op jit(solution)/shard_map/ppermute | solution.py:17
  37.1 1.5 %copy-start.4 = (bf16[1156,768]{1,0:T(8,128)(2,1)S(1)}, bf16[1156,768]{1,0:T(8,128)(2,1)}, u32[]{:S(2)}) copy-start(bf16[1156,768]{1,0:T(8,128)(2,1)} %reshape.129) | copy-start | bytes 5326852
  38.5 1.5 %copy-start.2 = (bf16[1156,768]{1,0:T(8,128)(2,1)S(1)}, bf16[1156,768]{1,0:T(8,128)(2,1)}, u32[]{:S(2)}) copy-start(bf16[1156,768]{1,0:T(8,128)(2,1)} %reshape.130) | copy-start | bytes 5326852
  38.6 1.5 %copy-start.11 = (bf16[1,1,3,256,256]{4,3,2,1,0:T(8,128)(2,1)S(1)}, bf16[1,1,3,256,256]{4,3,2,1,0:T(8,128)(2,1)}, u32[]{:S(2)}) copy-start(bf16[1,1,3,256,256]{4,3,2,1,0:T(8,128)(2,1)} %get-tuple-element.20) | copy-start | bytes 1179652
  41.8 1.0 copy-start.5
  42.4 1.0 copy-start.9
  43.5 1.0 copy-start.7
  45.0 28.5 %copy-start.17 = (bf16[32,32,256]{2,1,0:T(8,128)(2,1)S(1)}, bf16[32,32,256]{2,1,0:T(8,128)(2,1)}, u32[]{:S(2)}) copy-start(bf16[32,32,256]{2,1,0:T(8,128)(2,1)} %param.7) | copy-start | bytes 1572868
  45.3 28.3 %collective-permute-start.4 = (bf16[32,32,256]{2,1,0:T(8,128)(2,1)S(1)}, bf16[32,32,256]{2,1,0:T(8,128)(2,1)}, u32[]{:S(2)}, u32[]{:S(2)}) collective-permute-start(bf16[32,32,256]{2,1,0:T(8,128)(2,1)S(1)} %maximum_convert_fusion.1), channel_id=1, source_target_pairs={{0,128},{128,256},{256,384},{1,129},{129,257},{257,385},{2,130},{1... | collective-permute-start | bytes 1572872 | tf_op jit(solution)/shard_map/ppermute | solution.py:25
  74.7 4.3 %collective-permute-start.5 = (bf16[2,32,256]{2,1,0:T(8,128)(2,1)S(1)}, bf16[2,32,256]{2,1,0:T(8,128)(2,1)S(1)}, u32[]{:S(2)}, u32[]{:S(2)}) collective-permute-start(bf16[2,32,256]{2,1,0:T(8,128)(2,1)S(1)} %get-tuple-element.33), channel_id=1, source_target_pairs={{0,32},{32,64},{64,96},{1,33},{33,65},{65,97},{2,34},{34,66},{66,9... | collective-permute-start | bytes 98312 | tf_op jit(solution)/shard_map/ppermute | solution.py:14
  76.9 5.2 %collective-permute-start.6 = (bf16[2,32,256]{2,1,0:T(8,128)(2,1)S(1)}, bf16[2,32,256]{2,1,0:T(8,128)(2,1)S(1)}, u32[]{:S(2)}, u32[]{:S(2)}) collective-permute-start(bf16[2,32,256]{2,1,0:T(8,128)(2,1)S(1)} %get-tuple-element.34), channel_id=1, source_target_pairs={{32,0},{64,32},{96,64},{33,1},{65,33},{97,65},{34,2},{66,34},{98,6... | collective-permute-start | bytes 98312 | tf_op jit(solution)/shard_map/ppermute | solution.py:17
  82.2 6.5 %collective-permute-start.7 = (bf16[36,2,256]{2,1,0:T(2,128)(2,1)S(1)}, bf16[36,2,256]{2,1,0:T(2,128)(2,1)S(1)}, u32[]{:S(2)}, u32[]{:S(2)}) collective-permute-start(bf16[36,2,256]{2,1,0:T(2,128)(2,1)S(1)} %get-tuple-element.29), channel_id=1, source_target_pairs={{0,1},{1,2},{2,3},{3,4},{4,5},{5,6},{6,7},{7,8},{8,9},{9,10},{10,1... | collective-permute-start | bytes 110600 | tf_op jit(solution)/shard_map/ppermute | solution.py:14
  84.1 8.0 %collective-permute-start.8 = (bf16[36,2,256]{2,1,0:T(2,128)(2,1)S(1)}, bf16[36,2,256]{2,1,0:T(2,128)(2,1)S(1)}, u32[]{:S(2)}, u32[]{:S(2)}) collective-permute-start(bf16[36,2,256]{2,1,0:T(2,128)(2,1)S(1)} %get-tuple-element.30), channel_id=1, source_target_pairs={{1,0},{2,1},{3,2},{4,3},{5,4},{6,5},{7,6},{8,7},{9,8},{10,9},{11,1... | collective-permute-start | bytes 110600 | tf_op jit(solution)/shard_map/ppermute | solution.py:17
  106.0 1.5 %copy-start.3 = (bf16[1156,768]{1,0:T(8,128)(2,1)S(1)}, bf16[1156,768]{1,0:T(8,128)(2,1)}, u32[]{:S(2)}) copy-start(bf16[1156,768]{1,0:T(8,128)(2,1)} %reshape.138) | copy-start | bytes 5326852
  106.0 1.5 %copy-start.14 = (bf16[1,1,3,256,256]{4,3,2,1,0:T(8,128)(2,1)S(1)}, bf16[1,1,3,256,256]{4,3,2,1,0:T(8,128)(2,1)}, u32[]{:S(2)}) copy-start(bf16[1,1,3,256,256]{4,3,2,1,0:T(8,128)(2,1)} %copy-done.13) | copy-start | bytes 1179652
  107.5 1.5 %copy-start.1 = (bf16[1156,768]{1,0:T(8,128)(2,1)S(1)}, bf16[1156,768]{1,0:T(8,128)(2,1)}, u32[]{:S(2)}) copy-start(bf16[1156,768]{1,0:T(8,128)(2,1)} %reshape.139) | copy-start | bytes 5326852
  107.5 1.5 %copy-start.12 = (bf16[1,1,3,256,256]{4,3,2,1,0:T(8,128)(2,1)S(1)}, bf16[1,1,3,256,256]{4,3,2,1,0:T(8,128)(2,1)}, u32[]{:S(2)}) copy-start(bf16[1,1,3,256,256]{4,3,2,1,0:T(8,128)(2,1)} %get-tuple-element.20) | copy-start | bytes 1179652
  113.1 1.0 copy-start.6
  113.7 1.0 copy-start.10
  114.7 1.0 copy-start.8
  116.3 1.0 copy-start.15
where the time goes:
time: 119 us; the launch traced here: 118 us
  waiting for transfers between devices  34.8 us (29%)
  local copies, waits for them, and re-layouts  34.4 us (29%)
  starting transfers between devices  28.6 us (24%)
  other arithmetic  11.6 us (10%)
  matrix products  8.47 us (7%)
    ppermute x1, waiting for transfers between devices, shifted(): return lax.ppermute(x, axis, pairs)  22.2 us
    reshape x6, local copies, waits for them, and re-layouts, convolve(): stacked[row_tap:row_tap + out_rows]  16.1 us
    ppermute x4, starting transfers between devices, extended(): lax.ppermute(lax.slice_in_dim(block, block.shape[dim] - width, None, axis...  13 us
    ppermute x4, waiting for transfers between devices, extended(): lax.ppermute(lax.slice_in_dim(block, 0, width, axis=dim), axis, backward)  12.6 us
    ppermute x4, starting transfers between devices, extended(): lax.ppermute(lax.slice_in_dim(block, 0, width, axis=dim), axis, backward)  9.52 us
    dot_general x12, matrix products, convolve(): jnp.dot(stacked[row_tap:row_tap + out_rows].reshape(out_rows * out_cols,...  8.47 us
    concatenate x4, other arithmetic, convolve(): jnp.concatenate([padded[:, col_tap:col_tap + out_cols] for col_tap in ran...  7.06 us
    ppermute x1, starting transfers between devices, shifted(): return lax.ppermute(x, axis, pairs)  6.12 us
  transfers between devices with their start and end apart: 9, of which 4 were waited for; matrix products, arithmetic and copies ran while one was open for 4% of the time, Pallas kernels for 0%

commit v1 on v0

v1 whole, which is shorter than its diff:
```python
import functools

import jax
import jax.numpy as jnp
from jax import lax
from jax.experimental import pallas as pl
from jax.experimental.pallas import tpu as pltpu
from jax.sharding import PartitionSpec as P

TICKS = 2
BF16 = jnp.bfloat16
F32 = jnp.float32
BLOCK = 8


def edge_rows(x, axis_name):
    count = lax.axis_size(axis_name)
    forward = [(i, i + 1) for i in range(count - 1)]
    backward = [(target, source) for source, target in forward]
    low = lax.ppermute(x[-2:], axis_name, forward)
    high = lax.ppermute(x[:2], axis_name, backward)
    return low, high


def edge_cols(x, low, high, axis_name):
    count = lax.axis_size(axis_name)
    forward = [(i, i + 1) for i in range(count - 1)]
    backward = [(target, source) for source, target in forward]
    tall_right = jnp.concatenate([low[:, -2:], x[:, -2:], high[:, -2:]], axis=0)
    tall_left = jnp.concatenate([low[:, :2], x[:, :2], high[:, :2]], axis=0)
    left = lax.ppermute(tall_right, axis_name, forward)
    right = lax.ppermute(tall_left, axis_name, backward)
    return left, right


def shifted(x, axis, by):
    devices = lax.axis_size(axis)
    pairs = [(i, i + by) for i in range(devices) if 0 <= i + by < devices]
    return lax.ppermute(x, axis, pairs)


def tick_kernel(
    flags, x, top, bot, left, right, k1, k2, gains, shifts, out, x3, h3, edge, hedge, *, first, count
):
    rows, cols, chan = x.shape
    half = hedge.shape[0] // 2
    iota = lax.broadcasted_iota(jnp.int32, (cols, 1), 0)

    def stack(source, index, p):
        at = p - first
        wide = source[index]
        row = wide.astype(F32)
        lo = left[p].astype(F32)
        hi = right[p].astype(F32)
        spot = pl.multiple_of(at * cols, cols)
        x3[pl.ds(spot, cols), 0:chan] = jnp.where(iota == 0, lo[1:2], pltpu.roll(row, 1, 0)).astype(BF16)
        x3[pl.ds(spot, cols), chan : 2 * chan] = wide
        x3[pl.ds(spot, cols), 2 * chan :] = jnp.where(
            iota == cols - 1, hi[0:1], pltpu.roll(row, cols - 1, 0)
        ).astype(BF16)
        edge[pl.ds(at, 1), 0:chan] = lo[0:1]
        edge[pl.ds(at, 1), chan : 2 * chan] = lo[1:2]
        edge[pl.ds(at, 1), 2 * chan :] = row[0:1]
        edge[pl.ds(half + at, 1), 0:chan] = row[cols - 1 : cols]
        edge[pl.ds(half + at, 1), chan : 2 * chan] = hi[0:1]
        edge[pl.ds(half + at, 1), 2 * chan :] = hi[1:2]

    edge[...] = jnp.zeros(edge.shape, F32)
    for p in range(first, min(2, first + count + 4)):
        stack(top, p, p)
    start = max(first, 2)
    stop = min(first + count + 4, rows + 2)

    @pl.loop(start, stop)
    def _(p):
        stack(x, p - 2, p)

    for p in range(max(first, rows + 2), first + count + 4):
        stack(bot, p - rows - 2, p)

    gain1, shift1 = gains[0:1], shifts[0:1]
    gain2, shift2 = gains[1:2], shifts[1:2]
    wide_edge = edge[...].astype(BF16)
    total = None
    for tap in range(3):
        part = jnp.dot(wide_edge, k1[pl.ds(tap * 3 * chan, 3 * chan)], preferred_element_type=F32)
        if tap:
            part = pltpu.roll(part, 2 * half - tap, 0)
        total = part if total is None else total + part
    spots = lax.broadcasted_iota(jnp.int32, (2 * half, 1), 0)
    side = spots >= half
    hid_row = first - 1 + jnp.where(side, spots - half, spots)
    keep_row = ((hid_row >= 0) | (flags[0] == 0)) & ((hid_row < rows) | (flags[1] == 0))
    keep_col = (side & (flags[3] == 0)) | (jnp.logical_not(side) & (flags[2] == 0))
    hedge[...] = jnp.where(keep_row & keep_col, jnp.maximum(gain1 * total + shift1, 0.0), 0.0)

    def hidden_block(i, size):
        spot = pl.multiple_of(i * cols, cols)
        acc = None
        for tap in range(3):
            part = jnp.dot(
                x3[pl.ds(spot + tap * cols, size * cols), :],
                k1[pl.ds(tap * 3 * chan, 3 * chan)],
                preferred_element_type=F32,
            )
            acc = part if acc is None else acc + part
        acc = jnp.maximum(gain1 * acc + shift1, 0.0)
        for r in range(size):
            row_id = first - 1 + i + r
            keep = ((row_id >= 0) | (flags[0] == 0)) & ((row_id < rows) | (flags[1] == 0))
            row = jnp.where(keep, acc[r * cols : (r + 1) * cols], 0.0)
            lo = hedge[pl.ds(i + r, 1)]
            hi = hedge[pl.ds(half + i + r, 1)]
            here = pl.ds(spot + r * cols, cols)
            h3[here, 0:chan] = jnp.where(iota == 0, lo, pltpu.roll(row, 1, 0)).astype(BF16)
            h3[here, chan : 2 * chan] = row.astype(BF16)
            h3[here, 2 * chan :] = jnp.where(iota == cols - 1, hi, pltpu.roll(row, cols - 1, 0)).astype(BF16)

    def output_block(i, size):
        spot = pl.multiple_of(i * cols, cols)
        acc = None
        for tap in range(3):
            part = jnp.dot(
                h3[pl.ds(spot + tap * cols, size * cols), :],
                k2[pl.ds(tap * 3 * chan, 3 * chan)],
                preferred_element_type=F32,
            )
            acc = part if acc is None else acc + part
        acc = (gain2 * acc + shift2).reshape(size, cols, chan)
        base = x[pl.ds(first + i, size)].astype(F32)
        out[pl.ds(i, size)] = jnp.maximum(base + acc, 0.0).astype(BF16)

    def blocks(total_rows, body):
        whole = total_rows // BLOCK

        @pl.loop(0, whole)
        def _(b):
            body(b * BLOCK, BLOCK)

        if total_rows % BLOCK:
            body(whole * BLOCK, total_rows % BLOCK)

    blocks(count + 2, hidden_block)
    blocks(count, output_block)


def tick_call(flags, x, low, high, left, right, k1, k2, gains, shifts, first, count):
    rows, cols, chan = x.shape
    half = -(-(count + 4) // 8) * 8
    vmem = pl.BlockSpec(memory_space=pltpu.VMEM)
    return pl.pallas_call(
        functools.partial(tick_kernel, first=first, count=count),
        out_shape=jax.ShapeDtypeStruct((count, cols, chan), BF16),
        in_specs=[pl.BlockSpec(memory_space=pltpu.SMEM)] + [vmem] * 9,
        out_specs=vmem,
        scratch_shapes=[
            pltpu.VMEM(((count + 4) * cols, 3 * chan), BF16),
            pltpu.VMEM(((count + 2) * cols, 3 * chan), BF16),
            pltpu.VMEM((2 * half, 3 * chan), F32),
            pltpu.VMEM((2 * half, chan), F32),
        ],
        compiler_params=pltpu.CompilerParams(vmem_limit_bytes=24 * 1024 * 1024),
        name=f"tick_{first}_{count}",
    )(flags, x, low, high, left, right, k1, k2, gains, shifts)


def per_device(state, fresh, conv_first, conv_second, gains, shifts):
    chan = state.shape[-1]
    k1 = conv_first[0].reshape(9 * chan, chan)
    k2 = conv_second[0].reshape(9 * chan, chan)
    row, col = lax.axis_index("row"), lax.axis_index("col")
    flags = jnp.stack(
        [row == 0, row == lax.axis_size("row") - 1, col == 0, col == lax.axis_size("col") - 1]
    ).astype(jnp.int32)
    features = state[0]
    results = []
    for tick_index in range(TICKS):
        low, high = edge_rows(features, "row")
        left, right = edge_cols(features, low, high, "col")
        output = tick_call(
            flags, features, low, high, left, right, k1, k2, gains[0], shifts[0], 0, features.shape[0]
        )
        results.append(output)
        if tick_index + 1 < TICKS:
            arrived = shifted(output, "section", 1)
            features = jnp.where(lax.axis_index("section") == 0, fresh, arrived)
    return jnp.stack(results)[:, None]


def solution(mesh):
    in_specs = (
        P("section", "row", "col", None),
        P("row", "col", None),
        P("section", None, None, None, None),
        P("section", None, None, None, None),
        P("section", None, None),
        P("section", None, None),
    )
    out_specs = P(None, "section", "row", "col", None)
    return jax.shard_map(
        per_device, mesh=mesh, in_specs=in_specs, out_specs=out_specs, check_vma=False
    )
```

time: 119 us -> 86.1 us (0.72)
  the two profiles are of different devices: /device:TPU:159 before, /device:TPU:478 now
where the time goes in v1:
time: 86.1 us; the launch traced here: 85.4 us
  waiting for transfers between devices  38.6 us (45%)
  starting transfers between devices  25.8 us (30%)
  Pallas kernels  11.5 us (13%)
  local copies, waits for them, and re-layouts  6.87 us (8%)
  other arithmetic  2.5 us (3%)
    ppermute x1, waiting for transfers between devices, shifted(): return lax.ppermute(x, axis, pairs)  21.1 us
    ppermute x2, waiting for transfers between devices, edge_cols(): right = lax.ppermute(tall_left, axis_name, backward)  12.4 us
    pallas_call x2, Pallas kernels, tick_call(): pl.pallas_call(functools.partial(tick_kernel, first=first, count=count),...  11.5 us
    ppermute x2, starting transfers between devices, edge_rows(): high = lax.ppermute(x[:2], axis_name, backward)  7.7 us
    ppermute x2, starting transfers between devices, edge_cols(): left = lax.ppermute(tall_right, axis_name, forward)  6.53 us
    ppermute x2, starting transfers between devices, edge_cols(): right = lax.ppermute(tall_left, axis_name, backward)  5.84 us
    ppermute x2, waiting for transfers between devices, edge_rows(): low = lax.ppermute(x[-2:], axis_name, forward)  5.03 us
    unnamed x20, local copies, waits for them, and re-layouts  4.97 us
  transfers between devices with their start and end apart: 9, of which 5 were waited for; matrix products, arithmetic and copies ran while one was open for 2% of the time, Pallas kernels for 0%

profile of v1, /device:TPU:478, one launch (start us, length us, event | category | flops | bytes accessed | tf_op | source)
XLA Modules:
  0.0 85.4 jit_solution(7935947639624787808)
XLA Ops:
  0.0 0.8 slice_bitcast_fusion
  0.8 1.9 %collective-permute-start.1 = (bf16[2,32,256]{2,1,0:T(8,128)(2,1)S(1)}, bf16[2,32,256]{2,1,0:T(8,128)(2,1)S(1)}, u32[]{:S(2)}, u32[]{:S(2)}) collective-permute-start(bf16[2,32,256]{2,1,0:T(8,128)(2,1)S(1)} %get-tuple-element.11), channel_id=1, source_target_pairs={{32,0},{64,32},{96,64},{33,1},{65,33},{97,65},{34,2},{66,34},{98,6... | collective-permute-start | bytes 98312 | tf_op jit(solution)/shard_map/ppermute | solution.py:21
  2.7 2.4 %collective-permute-start = (bf16[2,32,256]{2,1,0:T(8,128)(2,1)S(1)}, bf16[2,32,256]{2,1,0:T(8,128)(2,1)S(1)}, u32[]{:S(2)}, u32[]{:S(2)}) collective-permute-start(bf16[2,32,256]{2,1,0:T(8,128)(2,1)S(1)} %get-tuple-element.12), channel_id=1, source_target_pairs={{0,32},{32,64},{64,96},{1,33},{33,65},{65,97},{2,34},{34,66},{66,9... | collective-permute-start | bytes 98312 | tf_op jit(solution)/shard_map/ppermute | solution.py:20
  5.1 1.0 %fusion.2 = (bf16[32,2,256]{2,1,0:T(2,128)(2,1)S(1)}, bf16[32,2,256]{2,1,0:T(2,128)(2,1)S(1)}) fusion(bf16[32,32,256]{2,1,0:T(8,128)(2,1)} %bitcast.25), kind=kLoop, calls=%fused_computation.11 | loop fusion | bytes 131072 | tf_op jit(solution)/shard_map/slice | solution.py:30
  6.2 0.0 collective-permute-done.1.bot
  6.2 1.8 %collective-permute-done.top = bf16[2,32,256]{2,1,0:T(8,128)(2,1)S(1)} collective-permute-done((bf16[2,32,256]{2,1,0:T(8,128)(2,1)S(1)}, bf16[2,32,256]{2,1,0:T(8,128)(2,1)S(1)}, u32[]{:S(2)}, u32[]{:S(2)}) %collective-permute-start) | collective-permute-done | bytes 32800 | tf_op jit(solution)/shard_map/ppermute | solution.py:20
  7.9 0.1 pad_maximum_fusion
  8.0 4.6 %collective-permute-start.2 = (bf16[36,2,256]{2,1,0:T(2,128)(2,1)S(1)}, bf16[36,2,256]{2,1,0:T(2,128)(2,1)S(1)}, u32[]{:S(2)}, u32[]{:S(2)}) collective-permute-start(bf16[36,2,256]{2,1,0:T(2,128)(2,1)S(1)} %pad_maximum_fusion), channel_id=1, source_target_pairs={{0,1},{1,2},{2,3},{3,4},{4,5},{5,6},{6,7},{7,8},{8,9},{9,10},{10,1... | collective-permute-start | bytes 110600 | tf_op jit(solution)/shard_map/ppermute | solution.py:31
  12.6 0.1 pad_maximum_fusion.1
  12.7 1.9 %collective-permute-start.3 = (bf16[36,2,256]{2,1,0:T(2,128)(2,1)S(1)}, bf16[36,2,256]{2,1,0:T(2,128)(2,1)S(1)}, u32[]{:S(2)}, u32[]{:S(2)}) collective-permute-start(bf16[36,2,256]{2,1,0:T(2,128)(2,1)S(1)} %pad_maximum_fusion.1), channel_id=1, source_target_pairs={{1,0},{2,1},{3,2},{4,3},{5,4},{6,5},{7,6},{8,7},{9,8},{10,9},{11,1... | collective-permute-start | bytes 110600 | tf_op jit(solution)/shard_map/ppermute | solution.py:32
  14.6 0.1 add_convert_fusion.flags
  14.7 0.0 collective-permute-done.2.left
  14.7 7.2 %collective-permute-done.3.right = bf16[36,2,256]{2,1,0:T(2,128)(2,1)S(1)} collective-permute-done((bf16[36,2,256]{2,1,0:T(2,128)(2,1)S(1)}, bf16[36,2,256]{2,1,0:T(2,128)(2,1)S(1)}, u32[]{:S(2)}, u32[]{:S(2)}) %collective-permute-start.3) | collective-permute-done | bytes 36896 | tf_op jit(solution)/shard_map/ppermute | solution.py:32
  21.9 0.0 copy-start
  21.9 1.3 %copy-done = bf16[1,3,3,256,256]{4,3,2,1,0:T(8,128)(2,1)S(1)} copy-done((bf16[1,3,3,256,256]{4,3,2,1,0:T(8,128)(2,1)S(1)}, bf16[1,3,3,256,256]{4,3,2,1,0:T(8,128)(2,1)}, u32[]{:S(2)}) %copy-start) | copy-done | bytes 1179672
  23.1 0.0 copy-start.2
  23.1 1.3 %copy-done.2 = bf16[1,3,3,256,256]{4,3,2,1,0:T(8,128)(2,1)S(1)} copy-done((bf16[1,3,3,256,256]{4,3,2,1,0:T(8,128)(2,1)S(1)}, bf16[1,3,3,256,256]{4,3,2,1,0:T(8,128)(2,1)}, u32[]{:S(2)}) %copy-start.2) | copy-done | bytes 1179672
  24.4 0.0 copy-start.4
  24.4 1.0 %copy-done.4 = bf16[1,32,32,256]{3,2,1,0:T(8,128)(2,1)S(1)} copy-done((bf16[1,32,32,256]{3,2,1,0:T(8,128)(2,1)S(1)}, bf16[1,32,32,256]{3,2,1,0:T(8,128)(2,1)}, u32[]{:S(2)}) %copy-start.4) | copy-done | bytes 524312
  25.4 0.0 copy-start.5
  25.4 0.7 copy-done.5
  26.1 0.0 copy-start.7
  26.1 0.7 copy-done.7
  26.8 0.0 copy-start.9
  26.8 0.0 copy-start.3
  26.8 5.8 %tick_0_32.2 = bf16[32,32,256]{2,1,0:T(8,128)(2,1)S(1)} custom-call(s32[4]{0:T(128)S(1)} %add_convert_fusion.flags, bf16[32,32,256]{2,1,0:T(8,128)(2,1)S(1)} %bitcast.26, bf16[2,32,256]{2,1,0:T(8,128)(2,1)S(1)} %collective-permute-done.top, bf16[2,32,256]{2,1,0:T(8,128)(2,1)S(1)} %collective-permute-done.1.bot, ...), custom_call_target="tpu_custom_call" | custom-call | tf_op jit(solution)/shard_map/tick_0_32/pallas_call | solution.py:151
  32.6 0.0 copy-start.1
  32.6 0.0 copy-start.6
  32.6 0.0 copy-start.8
  32.6 1.4 %collective-permute-start.4 = (bf16[32,32,256]{2,1,0:T(8,128)(2,1)S(1)}, bf16[32,32,256]{2,1,0:T(8,128)(2,1)}, u32[]{:S(2)}, u32[]{:S(2)}) collective-permute-start(bf16[32,32,256]{2,1,0:T(8,128)(2,1)S(1)} %tick_0_32.2), channel_id=1, source_target_pairs={{0,128},{128,256},{256,384},{1,129},{129,257},{257,385},{2,130},{1... | collective-permute-start | bytes 1572872 | tf_op jit(solution)/shard_map/ppermute | solution.py:39
  34.0 21.1 %collective-permute-done.4 = bf16[32,32,256]{2,1,0:T(8,128)(2,1)} collective-permute-done((bf16[32,32,256]{2,1,0:T(8,128)(2,1)S(1)}, bf16[32,32,256]{2,1,0:T(8,128)(2,1)}, u32[]{:S(2)}, u32[]{:S(2)}) %collective-permute-start.4) | collective-permute-done | bytes 524320 | tf_op jit(solution)/shard_map/ppermute | solution.py:39
  55.2 0.0 copy-done.9
  55.2 1.1 %broadcast_select_fusion.x = bf16[32,32,256]{2,1,0:T(8,128)(2,1)S(1)} fusion(bf16[32,32,256]{2,1,0:T(8,128)(2,1)S(1)} %copy-done.9, bf16[32,32,256]{2,1,0:T(8,128)(2,1)} %collective-permute-done.4, pred[]{:T(512)S(6)} %eq.19), kind=kLoop, calls=%fused_computation.1 | loop fusion | flops 262144 | bytes 1572865 | tf_op jit(solution)/shard_map/jit(_where)/select_n | solution.py:186
  56.3 5.8 %collective-permute-start.6 = (bf16[2,32,256]{2,1,0:T(8,128)(2,1)S(1)}, bf16[2,32,256]{2,1,0:T(8,128)(2,1)S(1)}, u32[]{:S(2)}, u32[]{:S(2)}) collective-permute-start(bf16[2,32,256]{2,1,0:T(8,128)(2,1)S(1)} %get-tuple-element.7), channel_id=1, source_target_pairs={{32,0},{64,32},{96,64},{33,1},{65,33},{97,65},{34,2},{66,34},{98,6... | collective-permute-start | bytes 98312 | tf_op jit(solution)/shard_map/ppermute | solution.py:21
  62.1 0.1 fusion
  62.2 1.9 %collective-permute-start.5 = (bf16[2,32,256]{2,1,0:T(8,128)(2,1)S(1)}, bf16[2,32,256]{2,1,0:T(8,128)(2,1)S(1)}, u32[]{:S(2)}, u32[]{:S(2)}) collective-permute-start(bf16[2,32,256]{2,1,0:T(8,128)(2,1)S(1)} %get-tuple-element.8), channel_id=1, source_target_pairs={{0,32},{32,64},{64,96},{1,33},{33,65},{65,97},{2,34},{34,66},{66,9... | collective-permute-start | bytes 98312 | tf_op jit(solution)/shard_map/ppermute | solution.py:20
  64.1 0.0 collective-permute-done.6.bot
  64.1 3.3 %collective-permute-done.5.top = bf16[2,32,256]{2,1,0:T(8,128)(2,1)S(1)} collective-permute-done((bf16[2,32,256]{2,1,0:T(8,128)(2,1)S(1)}, bf16[2,32,256]{2,1,0:T(8,128)(2,1)S(1)}, u32[]{:S(2)}, u32[]{:S(2)}) %collective-permute-start.5) | collective-permute-done | bytes 32800 | tf_op jit(solution)/shard_map/ppermute | solution.py:20
  67.4 0.1 pad_maximum_fusion.2
  67.5 1.9 %collective-permute-start.7 = (bf16[36,2,256]{2,1,0:T(2,128)(2,1)S(1)}, bf16[36,2,256]{2,1,0:T(2,128)(2,1)S(1)}, u32[]{:S(2)}, u32[]{:S(2)}) collective-permute-start(bf16[36,2,256]{2,1,0:T(2,128)(2,1)S(1)} %pad_maximum_fusion.2), channel_id=1, source_target_pairs={{0,1},{1,2},{2,3},{3,4},{4,5},{5,6},{6,7},{7,8},{8,9},{9,10},{10,1... | collective-permute-start | bytes 110600 | tf_op jit(solution)/shard_map/ppermute | solution.py:31
  69.4 0.1 pad_maximum_fusion.3
  69.5 3.9 %collective-permute-start.8 = (bf16[36,2,256]{2,1,0:T(2,128)(2,1)S(1)}, bf16[36,2,256]{2,1,0:T(2,128)(2,1)S(1)}, u32[]{:S(2)}, u32[]{:S(2)}) collective-permute-start(bf16[36,2,256]{2,1,0:T(2,128)(2,1)S(1)} %pad_maximum_fusion.3), channel_id=1, source_target_pairs={{1,0},{2,1},{3,2},{4,3},{5,4},{6,5},{7,6},{8,7},{9,8},{10,9},{11,1... | collective-permute-start | bytes 110600 | tf_op jit(solution)/shard_map/ppermute | solution.py:32
  73.4 0.0 collective-permute-done.7.left
  73.4 5.2 %collective-permute-done.8.right = bf16[36,2,256]{2,1,0:T(2,128)(2,1)S(1)} collective-permute-done((bf16[36,2,256]{2,1,0:T(2,128)(2,1)S(1)}, bf16[36,2,256]{2,1,0:T(2,128)(2,1)S(1)}, u32[]{:S(2)}, u32[]{:S(2)}) %collective-permute-start.8) | collective-permute-done | bytes 36896 | tf_op jit(solution)/shard_map/ppermute | solution.py:32
  78.6 0.0 copy-done.3
  78.6 0.0 copy-done.1
  78.6 0.0 copy-done.6
  78.7 0.0 copy-done.8
  78.7 5.7 %tick_0_32.3 = bf16[32,32,256]{2,1,0:T(8,128)(2,1)S(1)} custom-call(s32[4]{0:T(128)S(1)} %add_convert_fusion.flags, bf16[32,32,256]{2,1,0:T(8,128)(2,1)S(1)} %broadcast_select_fusion.x, bf16[2,32,256]{2,1,0:T(8,128)(2,1)S(1)} %collective-permute-done.5.top, bf16[2,32,256]{2,1,0:T(8,128)(2,1)S(1)} %collective-permute-done.6.bot, ...), custom_call_target="tpu_custom_call" | custom-call | tf_op jit(solution)/shard_map/tick_0_32/pallas_call | solution.py:151
  84.4 1.1 %maximum_bitcast_fusion = bf16[2,1,32,32,256]{4,3,2,1,0:T(8,128)(2,1)} fusion(bf16[1,32,32,256]{3,2,1,0:T(8,128)(2,1)S(1)} %bitcast.24, bf16[1,32,32,256]{3,2,1,0:T(8,128)(2,1)S(1)} %bitcast.23), kind=kLoop, calls=%fused_computation | loop fusion | flops 524288 | bytes 2097152 | tf_op jit(solution)/shard_map/broadcast_in_dim | solution.py:187
  (5 shorter events, 0.0 us)
Async XLA Ops:
  0.8 5.4 %collective-permute-start.1 = (bf16[2,32,256]{2,1,0:T(8,128)(2,1)S(1)}, bf16[2,32,256]{2,1,0:T(8,128)(2,1)S(1)}, u32[]{:S(2)}, u32[]{:S(2)}) collective-permute-start(bf16[2,32,256]{2,1,0:T(8,128)(2,1)S(1)} %get-tuple-element.11), channel_id=1, source_target_pairs={{32,0},{64,32},{96,64},{33,1},{65,33},{97,65},{34,2},{66,34},{98,6... | collective-permute-start | bytes 98312 | tf_op jit(solution)/shard_map/ppermute | solution.py:21
  2.7 5.2 %collective-permute-start = (bf16[2,32,256]{2,1,0:T(8,128)(2,1)S(1)}, bf16[2,32,256]{2,1,0:T(8,128)(2,1)S(1)}, u32[]{:S(2)}, u32[]{:S(2)}) collective-permute-start(bf16[2,32,256]{2,1,0:T(8,128)(2,1)S(1)} %get-tuple-element.12), channel_id=1, source_target_pairs={{0,32},{32,64},{64,96},{1,33},{33,65},{65,97},{2,34},{34,66},{66,9... | collective-permute-start | bytes 98312 | tf_op jit(solution)/shard_map/ppermute | solution.py:20
  8.0 6.7 %collective-permute-start.2 = (bf16[36,2,256]{2,1,0:T(2,128)(2,1)S(1)}, bf16[36,2,256]{2,1,0:T(2,128)(2,1)S(1)}, u32[]{:S(2)}, u32[]{:S(2)}) collective-permute-start(bf16[36,2,256]{2,1,0:T(2,128)(2,1)S(1)} %pad_maximum_fusion), channel_id=1, source_target_pairs={{0,1},{1,2},{2,3},{3,4},{4,5},{5,6},{6,7},{7,8},{8,9},{9,10},{10,1... | collective-permute-start | bytes 110600 | tf_op jit(solution)/shard_map/ppermute | solution.py:31
  12.7 9.2 %collective-permute-start.3 = (bf16[36,2,256]{2,1,0:T(2,128)(2,1)S(1)}, bf16[36,2,256]{2,1,0:T(2,128)(2,1)S(1)}, u32[]{:S(2)}, u32[]{:S(2)}) collective-permute-start(bf16[36,2,256]{2,1,0:T(2,128)(2,1)S(1)} %pad_maximum_fusion.1), channel_id=1, source_target_pairs={{1,0},{2,1},{3,2},{4,3},{5,4},{6,5},{7,6},{8,7},{9,8},{10,9},{11,1... | collective-permute-start | bytes 110600 | tf_op jit(solution)/shard_map/ppermute | solution.py:32
  21.9 1.3 %copy-start = (bf16[1,3,3,256,256]{4,3,2,1,0:T(8,128)(2,1)S(1)}, bf16[1,3,3,256,256]{4,3,2,1,0:T(8,128)(2,1)}, u32[]{:S(2)}) copy-start(bf16[1,3,3,256,256]{4,3,2,1,0:T(8,128)(2,1)} %param.8) | copy-start | bytes 3538948
  23.1 1.3 %copy-start.2 = (bf16[1,3,3,256,256]{4,3,2,1,0:T(8,128)(2,1)S(1)}, bf16[1,3,3,256,256]{4,3,2,1,0:T(8,128)(2,1)}, u32[]{:S(2)}) copy-start(bf16[1,3,3,256,256]{4,3,2,1,0:T(8,128)(2,1)} %param.9) | copy-start | bytes 3538948
  24.4 1.0 %copy-start.4 = (bf16[1,32,32,256]{3,2,1,0:T(8,128)(2,1)S(1)}, bf16[1,32,32,256]{3,2,1,0:T(8,128)(2,1)}, u32[]{:S(2)}) copy-start(bf16[1,32,32,256]{3,2,1,0:T(8,128)(2,1)} %param.6) | copy-start | bytes 1572868
  25.4 0.7 copy-start.5
  26.1 0.7 copy-start.7
  26.8 28.4 %copy-start.9 = (bf16[32,32,256]{2,1,0:T(8,128)(2,1)S(1)}, bf16[32,32,256]{2,1,0:T(8,128)(2,1)}, u32[]{:S(2)}) copy-start(bf16[32,32,256]{2,1,0:T(8,128)(2,1)} %param.7) | copy-start | bytes 1572868
  26.8 51.8 %copy-start.3 = (bf16[1,3,3,256,256]{4,3,2,1,0:T(8,128)(2,1)S(1)}, bf16[1,3,3,256,256]{4,3,2,1,0:T(8,128)(2,1)}, u32[]{:S(2)}) copy-start(bf16[1,3,3,256,256]{4,3,2,1,0:T(8,128)(2,1)} %param.9) | copy-start | bytes 3538948
  32.6 46.1 %copy-start.1 = (bf16[1,3,3,256,256]{4,3,2,1,0:T(8,128)(2,1)S(1)}, bf16[1,3,3,256,256]{4,3,2,1,0:T(8,128)(2,1)}, u32[]{:S(2)}) copy-start(bf16[1,3,3,256,256]{4,3,2,1,0:T(8,128)(2,1)} %param.8) | copy-start | bytes 3538948
  32.6 46.1 %copy-start.6 = (f32[1,2,256]{2,1,0:T(2,128)S(1)}, f32[1,2,256]{2,1,0:T(2,128)}, u32[]{:S(2)}) copy-start(f32[1,2,256]{2,1,0:T(2,128)} %param.10) | copy-start | bytes 6148
  32.6 46.1 %copy-start.8 = (f32[1,2,256]{2,1,0:T(2,128)S(1)}, f32[1,2,256]{2,1,0:T(2,128)}, u32[]{:S(2)}) copy-start(f32[1,2,256]{2,1,0:T(2,128)} %param.11) | copy-start | bytes 6148
  32.6 22.6 %collective-permute-start.4 = (bf16[32,32,256]{2,1,0:T(8,128)(2,1)S(1)}, bf16[32,32,256]{2,1,0:T(8,128)(2,1)}, u32[]{:S(2)}, u32[]{:S(2)}) collective-permute-start(bf16[32,32,256]{2,1,0:T(8,128)(2,1)S(1)} %tick_0_32.2), channel_id=1, source_target_pairs={{0,128},{128,256},{256,384},{1,129},{129,257},{257,385},{2,130},{1... | collective-permute-start | bytes 1572872 | tf_op jit(solution)/shard_map/ppermute | solution.py:39
  56.3 7.8 %collective-permute-start.6 = (bf16[2,32,256]{2,1,0:T(8,128)(2,1)S(1)}, bf16[2,32,256]{2,1,0:T(8,128)(2,1)S(1)}, u32[]{:S(2)}, u32[]{:S(2)}) collective-permute-start(bf16[2,32,256]{2,1,0:T(8,128)(2,1)S(1)} %get-tuple-element.7), channel_id=1, source_target_pairs={{32,0},{64,32},{96,64},{33,1},{65,33},{97,65},{34,2},{66,34},{98,6... | collective-permute-start | bytes 98312 | tf_op jit(solution)/shard_map/ppermute | solution.py:21
  62.2 5.2 %collective-permute-start.5 = (bf16[2,32,256]{2,1,0:T(8,128)(2,1)S(1)}, bf16[2,32,256]{2,1,0:T(8,128)(2,1)S(1)}, u32[]{:S(2)}, u32[]{:S(2)}) collective-permute-start(bf16[2,32,256]{2,1,0:T(8,128)(2,1)S(1)} %get-tuple-element.8), channel_id=1, source_target_pairs={{0,32},{32,64},{64,96},{1,33},{33,65},{65,97},{2,34},{34,66},{66,9... | collective-permute-start | bytes 98312 | tf_op jit(solution)/shard_map/ppermute | solution.py:20
  67.5 5.9 %collective-permute-start.7 = (bf16[36,2,256]{2,1,0:T(2,128)(2,1)S(1)}, bf16[36,2,256]{2,1,0:T(2,128)(2,1)S(1)}, u32[]{:S(2)}, u32[]{:S(2)}) collective-permute-start(bf16[36,2,256]{2,1,0:T(2,128)(2,1)S(1)} %pad_maximum_fusion.2), channel_id=1, source_target_pairs={{0,1},{1,2},{2,3},{3,4},{4,5},{5,6},{6,7},{7,8},{8,9},{9,10},{10,1... | collective-permute-start | bytes 110600 | tf_op jit(solution)/shard_map/ppermute | solution.py:31
  69.5 9.2 %collective-permute-start.8 = (bf16[36,2,256]{2,1,0:T(2,128)(2,1)S(1)}, bf16[36,2,256]{2,1,0:T(2,128)(2,1)S(1)}, u32[]{:S(2)}, u32[]{:S(2)}) collective-permute-start(bf16[36,2,256]{2,1,0:T(2,128)(2,1)S(1)} %pad_maximum_fusion.3), channel_id=1, source_target_pairs={{1,0},{2,1},{3,2},{4,3},{5,4},{6,5},{7,6},{8,7},{9,8},{10,9},{11,1... | collective-permute-start | bytes 110600 | tf_op jit(solution)/shard_map/ppermute | solution.py:32
